TPU v7x, 32 devices: a whole 2x2x4 slice. The times are simulated.
32 devices in a mesh: pp: 4 (over x, core), tp: 2 (over y), dp: 4 (over z).
Axes of the slice: x: 2, y: 2, z: 4, core: 2. Of those that a mesh axis runs over, the one named last changes fastest.
Arguments:
- layer_input: bfloat16 [4, 4, 16, 4096], P('pp', 'dp', 'tp'), may hold values from -4 to 4
- gate_pre: bfloat16 [4, 4, 16, 14784], P('pp', 'dp', None, 'tp'), may hold values from -8 to 8
- up_pre: bfloat16 [4, 4, 16, 14784], P('pp', 'dp', None, 'tp'), may hold values from -6 to 6
- hidden_grad: bfloat16 [4, 4, 16, 14784], P('pp', 'dp', None, 'tp'), may hold values from -0.59765625 to 0.59765625
- gate_weight: bfloat16 [4, 4096, 14784], P('pp', 'dp', 'tp'), may hold values from -0.09375 to 0.09375
Outputs:
- passed_grad: bfloat16 [4, 4, 16, 4096], P('pp', 'dp', 'tp')
- gate_weight_grad: bfloat16 [4, 4096, 14784], P('pp', 'dp', 'tp')
All inputs are finite; a program needn't handle non-finite values.
Results may differ from a plain program's by a relative error of at most 0.018.
Values may be sent and summed in bfloat16 or wider, within the bound.
A program may use at most 128 MiB of HBM per device.

v0:
```python
import jax
import jax.numpy as jnp
from jax import lax
from jax.sharding import PartitionSpec as P


def from_behind(block, axis, distance):
    devices = range(lax.axis_size(axis))
    route = [(i - distance, i) for i in devices if i - distance in devices]
    return lax.ppermute(block, axis, route)


def finish(partial_value):
    return lax.psum_scatter(
        partial_value.astype(jnp.bfloat16), "tp", scatter_dimension=0, tiled=True
    )


def on_device(layer_input, gate_pre, up_pre, hidden_grad, gate_weight):
    tokens_in = layer_input[0, 0]
    gate_val = gate_pre[0, 0].astype(jnp.float32)
    up_val = up_pre[0, 0].astype(jnp.float32)
    hidden_val = hidden_grad[0, 0].astype(jnp.float32)
    gate_local = gate_weight[0]
    rows_total = gate_val.shape[0]
    groups = lax.axis_size("dp")
    logistic = jax.nn.sigmoid(gate_val)
    gate_grad = (hidden_val * up_val * logistic * (1.0 + gate_val * (1.0 - logistic))).astype(
        jnp.bfloat16
    )
    gathered_in = lax.all_gather(tokens_in, "tp", axis=0, tiled=True)
    contract_cols = (((1,), (1,)), ((), ()))
    all_grads = lax.all_gather(gate_grad, "dp", axis=0, tiled=True)
    partial_value = lax.dot_general(
        all_grads, gate_local, contract_cols, preferred_element_type=jnp.float32
    )
    returned = lax.all_to_all(
        partial_value.astype(jnp.bfloat16), "dp", split_axis=0, concat_axis=1, tiled=True
    ).astype(partial_value.dtype)
    input_grad = finish(returned)
    in_columns = lax.all_to_all(gathered_in, "dp", split_axis=1, concat_axis=0, tiled=True)
    products = lax.dot_general(
        in_columns.reshape(groups, rows_total, in_columns.shape[1]),
        all_grads.reshape(groups, rows_total, all_grads.shape[1]),
        (((1,), (1,)), ((0,), (0,))),
        preferred_element_type=jnp.float32,
    )
    rounded = lax.optimization_barrier(products.astype(jnp.bfloat16))
    grads_total = jnp.sum(rounded.astype(jnp.float32), axis=0)
    passed = from_behind(input_grad, "pp", -1)
    gate_out = grads_total.astype(jnp.bfloat16)
    return (passed[None, None], gate_out[None])


def solution(mesh):
    return jax.shard_map(
        on_device,
        mesh=mesh,
        in_specs=(
            P("pp", "dp", "tp", None),
            P("pp", "dp", None, "tp"),
            P("pp", "dp", None, "tp"),
            P("pp", "dp", None, "tp"),
            P("pp", "dp", "tp"),
        ),
        out_specs=(P("pp", "dp", "tp", None), P("pp", "dp", "tp")),
        check_vma=False,
    )
```

profile of v0, /device:TPU:0, one launch (start us, length us, event | category | flops | bytes accessed | tf_op | source)
XLA Modules:
  0.0 123.4 jit_solution(5903681675003052307)
XLA Ops:
  7.2 0.0 copy-start
  7.2 0.0 reduce-scatter.2.cloned.1.call-start
  7.2 1.4 %fusion.10 = bf16[16,7392]{1,0:T(8,128)(2,1)S(1)} fusion(bf16[1,1,16,7392]{3,2,1,0:T(8,128)(2,1)} %param.7, bf16[1,1,16,7392]{3,2,1,0:T(8,128)(2,1)} %param.8, bf16[1,1,16,7392]{3,2,1,0:T(8,128)(2,1)} %param.6), kind=kLoop, calls=%fused_computation.11 | loop fusion | flops 1537536 | bytes 946176 | tf_op jit(solution)/shard_map/convert_element_type | solution.py:28
  8.6 23.1 %all_gather.6 = bf16[64,7392]{1,0:T(8,128)(2,1)S(1)} all-gather(bf16[16,7392]{1,0:T(8,128)(2,1)S(1)} %fusion.10), channel_id=1, replica_groups=mesh['pp'=4,'tp'=2,'dp'=4] {'dp'}, dimensions={0}, use_global_device_ids=true | all-gather | bytes 1182720 | tf_op jit(solution)/shard_map/all_gather | solution.py:33
  31.7 8.0 %fusion.2 = bf16[64,1024]{1,0:T(8,128)(2,1)S(1)} fusion(bf16[64,7392]{1,0:T(8,128)(2,1)S(1)} %all_gather.6, bf16[1,1024,7392]{1,2,0:T(8,128)(2,1)} %param.9), kind=kOutput, calls=%fused_computation.3 | convolution fusion | flops 968949760 | bytes 16216064 | tf_op jit(solution)/shard_map/dot_general | solution.py:34
  39.8 9.1 %all_to_all.35 = bf16[4,16,1024]{2,1,0:T(8,128)(2,1)S(1)} all-to-all(bf16[4,16,1024]{2,1,0:T(8,128)(2,1)S(1)} %bitcast.30), channel_id=1, replica_groups=mesh['pp'=4,'tp'=2,'dp'=4] {'dp'}, dimensions={0} | all-to-all | bytes 262144 | tf_op jit(solution)/shard_map/all_to_all | solution.py:37
  48.9 0.7 copy.10
  49.5 0.0 reduce-scatter.2.cloned.1.call-update
  49.6 0.0 copy-done
  49.6 4.9 %all-gather = bf16[1,1,16,4096]{3,2,1,0:T(8,128)(2,1)S(1)} all-gather(bf16[1,1,8,4096]{3,2,1,0:T(8,128)(2,1)S(1)} %copy-done), channel_id=2, replica_groups=mesh['pp'=4,'tp'=2,'dp'=4] {'tp'}, dimensions={2}, use_global_device_ids=true | all-gather | bytes 196608 | tf_op jit(solution)/shard_map/all_gather | solution.py:31
  54.5 0.1 all_to_all.30
  54.6 0.7 copy.9
  55.3 3.3 %all-to-all-start.1 = ((bf16[16,4,1024]{2,0,1:T(8,128)(2,1)}), bf16[16,4,1024]{2,0,1:T(8,128)(2,1)S(1)}, u32[]{:S(2)}, u32[]{:S(2)}) async-start(bf16[16,4,1024]{2,0,1:T(8,128)(2,1)} %copy.9), calls=%async_computation.2 | async-start | bytes 262144 | tf_op jit(solution)/shard_map/all_to_all | solution.py:41
  58.6 0.5 reduce-scatter.2.cloned.1.call-done
  59.1 1.3 %collective-permute-start = (bf16[8,4096]{1,0:T(8,128)(2,1)}, bf16[8,4096]{1,0:T(8,128)(2,1)S(1)}, u32[]{:S(2)}, u32[]{:S(2)}) collective-permute-start(bf16[8,4096]{1,0:T(8,128)(2,1)} %reduce-scatter.2.cloned.1.call-done), channel_id=1, source_target_pairs={{8,0},{16,8},{24,16},{9,1},{17,9},{25,17},{10,2},{18,10},{26,18},{... | collective-permute-start | bytes 196616 | tf_op jit(solution)/shard_map/ppermute | solution.py:10
  60.4 4.1 %all-to-all-done.1 = bf16[16,4,1024]{2,0,1:T(8,128)(2,1)S(1)} async-done(((bf16[16,4,1024]{2,0,1:T(8,128)(2,1)}), bf16[16,4,1024]{2,0,1:T(8,128)(2,1)S(1)}, u32[]{:S(2)}, u32[]{:S(2)}) %all-to-all-start.1) | async-done | bytes 131104 | tf_op jit(solution)/shard_map/all_to_all | solution.py:41
  64.5 23.4 %convert_bitcast_fusion = bf16[4,1024,7392]{1,2,0:T(8,128)(2,1)} fusion(bf16[4,16,7392]{2,1,0:T(8,128)(2,1)S(1)} %bitcast.28, bf16[16,4,1024]{2,0,1:T(8,128)(2,1)S(1)} %all-to-all-done.1), kind=kOutput, calls=%fused_computation | convolution fusion | flops 999161856 | bytes 61632512 | tf_op jit(solution)/shard_map/dot_general | solution.py:42
  87.9 28.0 %reduce_sum.12 = bf16[1024,7392]{0,1:T(8,128)(2,1)} reduce(bf16[4,1024,7392]{1,2,0:T(8,128)(2,1)} %convert_bitcast_fusion, bf16[]{:T(256)} %constant.4.clone.1), dimensions={0}, to_apply=%region_1.0 | reduce | flops 22708224 | bytes 75694080 | tf_op jit(solution)/shard_map/reduce_sum | solution.py:49
  115.9 0.0 collective-permute-done
  115.9 0.6 copy.12
Async XLA Ops:
  7.2 42.4 %copy-start = (bf16[1,1,8,4096]{3,2,1,0:T(8,128)(2,1)S(1)}, bf16[1,1,8,4096]{3,2,1,0:T(8,128)(2,1)}, u32[]{:S(2)}) copy-start(bf16[1,1,8,4096]{3,2,1,0:T(8,128)(2,1)} %param.5) | copy-start | bytes 196612
  7.2 51.9 %reduce-scatter.2.cloned.1.call-start = ((), (), s32[]{:S(2)}) async-start(), calls=%async_computation.3 | async-start | bytes 196608 | tf_op jit(solution)/shard_map/reduce_scatter | solution.py:14
  55.3 9.2 %all-to-all-start.1 = ((bf16[16,4,1024]{2,0,1:T(8,128)(2,1)}), bf16[16,4,1024]{2,0,1:T(8,128)(2,1)S(1)}, u32[]{:S(2)}, u32[]{:S(2)}) async-start(bf16[16,4,1024]{2,0,1:T(8,128)(2,1)} %copy.9), calls=%async_computation.2 | async-start | bytes 262144 | tf_op jit(solution)/shard_map/all_to_all | solution.py:41
  59.1 56.8 %collective-permute-start = (bf16[8,4096]{1,0:T(8,128)(2,1)}, bf16[8,4096]{1,0:T(8,128)(2,1)S(1)}, u32[]{:S(2)}, u32[]{:S(2)}) collective-permute-start(bf16[8,4096]{1,0:T(8,128)(2,1)} %reduce-scatter.2.cloned.1.call-done), channel_id=1, source_target_pairs={{8,0},{16,8},{24,16},{9,1},{17,9},{25,17},{10,2},{18,10},{26,18},{... | collective-permute-start | bytes 196616 | tf_op jit(solution)/shard_map/ppermute | solution.py:10
Sparse Core Ops, SparseCore 0:
  49.7 9.3 reduce-scatter.1
where the time goes:
time: 124 us; the launch traced here: 123 us
  blocking collectives  37.1 us (30%)
  matrix products  31.5 us (25%)
  other arithmetic  29.4 us (24%)
  between operations  14.1 us (11%)
  starting transfers between devices  4.64 us (4%)
  waiting for transfers between devices  4.62 us (4%)
  local copies, waits for them, and re-layouts  2.05 us (2%)
    reduce_sum x1, other arithmetic, on_device(): grads_total = jnp.sum(rounded.astype(jnp.float32), axis=0)  28 us
    dot_general x1, matrix products, on_device(): lax.dot_general(in_columns.reshape(groups, rows_total, in_columns.shape[1...  23.4 us
    all_gather x1, blocking collectives, on_device(): all_grads = lax.all_gather(gate_grad, 'dp', axis=0, tiled=True)  23.1 us
    all_to_all x1, blocking collectives, on_device(): lax.all_to_all(partial_value.astype(jnp.bfloat16), 'dp', split_axis=0, co...  9.09 us
    dot_general x1, matrix products, on_device(): lax.dot_general(all_grads, gate_local, contract_cols, preferred_element_t...  8.04 us
    all_gather x1, blocking collectives, on_device(): gathered_in = lax.all_gather(tokens_in, 'tp', axis=0, tiled=True)  4.93 us
    all_to_all x1, waiting for transfers between devices, on_device(): lax.all_to_all(gathered_in, 'dp', split_axis=1, concat_axis=0, tiled=True)  4.06 us
    all_to_all x1, starting transfers between devices, on_device(): lax.all_to_all(gathered_in, 'dp', split_axis=1, concat_axis=0, tiled=True)  3.32 us
  transfers between devices with their start and end apart: 3, of which 2 were waited for; matrix products, arithmetic and copies ran while one was open for 42% of the time, Pallas kernels for 0%

commit v1 on v0

v1 whole, which is shorter than its diff:
```python
import functools

import jax
import jax.numpy as jnp
from jax import lax
from jax.experimental import pallas as pl
from jax.experimental.pallas import tpu as pltpu
from jax.sharding import PartitionSpec as P

MESH = pl.DeviceIdType.MESH
LANES = 128


def chunk_list(width, tiles_each):
    bounds = list(range(0, width, tiles_each * LANES)) + [width]
    return list(zip(bounds[:-1], bounds[1:]))


def round_up(a, b):
    return (a + b - 1) // b * b


def gather_kernel(n_pp, n, m, chunks, x_hbm, g_hbm, u_hbm, h_hbm, w_hbm, g_out, x_out, passed_out, *scratch):
    (p_send, p_recv, pbuf, rbuf, xin, gin, uin, hin, wbuf, gbuf, xbuf, acc, in_sem, w_sem, out_sem, x_send, x_recv, xt_send, xt_recv,
     r_send, l_send, g_recv) = scratch
    p, d, t = lax.axis_index("pp"), lax.axis_index("dp"), lax.axis_index("tp")
    tokens, width = g_hbm.shape[2:]
    own_rows, feats = xbuf.shape[2:]
    padded = gbuf.shape[2]

    barrier = pltpu.get_barrier_semaphore()
    for i in range(1, n):
        pl.semaphore_signal(barrier, inc=1, device_id={"dp": lax.rem(d + i, n)}, device_id_type=MESH)
    for j in range(1, m):
        pl.semaphore_signal(barrier, inc=1, device_id={"tp": lax.rem(t + j, m)}, device_id_type=MESH)
    everyone = [(i, j) for j in range(m) for i in range(n)]

    def owner_of(stage, i, j):
        return {"pp": stage, "tp": lax.rem(t + j, m), "dp": lax.rem(d + i, n)}

    @pl.when(p > 0)
    def _():
        for i, j in everyone:
            pl.semaphore_signal(barrier, inc=1, device_id=owner_of(p - 1, i, j), device_id_type=MESH)

    @pl.when(p < n_pp - 1)
    def _():
        for i, j in everyone:
            pl.semaphore_signal(barrier, inc=1, device_id=owner_of(p + 1, i, j), device_id_type=MESH)


    loads = [
        pltpu.make_async_copy(src.at[0, 0], dst, in_sem.at[i])
        for i, (src, dst) in enumerate(((g_hbm, gin), (u_hbm, uin), (h_hbm, hin), (x_hbm, xin)))
    ]
    for load in loads:
        load.start()
    w_loads = []
    for c, (lo, hi) in enumerate(chunks):
        rows = pl.ds(lo, min(hi, width) - lo)
        whole = len(chunks) == 1
        source, target = (w_hbm.at[0], wbuf) if whole else (w_hbm.at[0, rows], wbuf.at[rows])
        w_loads.append(pltpu.make_async_copy(source, target, w_sem.at[c]))
        w_loads[c].start()
    acc[...] = jnp.zeros_like(acc)
    for load in loads[:3]:
        load.wait()
    if padded > width:
        last = padded - LANES
        gbuf[d, :, last:] = jnp.zeros((tokens, LANES), jnp.bfloat16)
    step_width = 4 * LANES
    for lo in range(0, width, step_width):
        hi = min(lo + step_width, width)
        gate = gin[:, lo:hi].astype(jnp.float32)
        up = uin[:, lo:hi].astype(jnp.float32)
        hidden = hin[:, lo:hi].astype(jnp.float32)
        sig = 1.0 / (1.0 + jnp.exp(-gate))
        gbuf[d, :, lo:hi] = (hidden * up * sig * (1.0 + gate * (1.0 - sig))).astype(jnp.bfloat16)
    loads[3].wait()
    sections = lax.div(p + n_pp - 1, n_pp) + lax.div(2 * n_pp - 2 - p, n_pp)
    pl.semaphore_wait(barrier, n - 1 + m - 1 + n * m * sections)

    x_copies = []
    for i in range(1, n):
        to = lax.rem(d + i, n)
        copy = pltpu.make_async_remote_copy(
            src_ref=xin.at[:, pl.ds(pl.multiple_of(to * feats, LANES), feats)],
            dst_ref=xbuf.at[t, d], send_sem=x_send.at[i], recv_sem=x_recv.at[d],
            device_id={"dp": to}, device_id_type=MESH)
        copy.start()
        x_copies.append(copy)
    x_local = pltpu.make_async_copy(
        xin.at[:, pl.ds(pl.multiple_of(d * feats, LANES), feats)], xbuf.at[t, d], out_sem.at[len(chunks)])
    x_local.start()

    def g_copy(block, c, to_right):
        lo, hi = chunks[c]
        cols = pl.ds(lo, min(hi, padded) - lo)
        sems = r_send if to_right else l_send
        return pltpu.make_async_remote_copy(
            src_ref=gbuf.at[block, :, cols], dst_ref=gbuf.at[block, :, cols],
            send_sem=sems.at[block, c], recv_sem=g_recv.at[block, c],
            device_id={"dp": d + 1 if to_right else d - 1}, device_id_type=MESH)

    x_tp = []
    for step in range(len(chunks) + n - 1):
        for k in range(n):
            c = step - k
            if c < 0 or c >= len(chunks):
                continue
            if k == 0:
                @pl.when(d < n - 1)
                def _():
                    g_copy(d, c, True).start()

                @pl.when(d > 0)
                def _():
                    g_copy(d, c, False).start()
            else:
                @pl.when(d - k >= 0)
                def _():
                    g_copy(d - k, c, True).wait_recv()

                    @pl.when(d < n - 1)
                    def _():
                        g_copy(d - k, c, True).start()

                @pl.when(d + k < n)
                def _():
                    g_copy(d + k, c, False).wait_recv()

                    @pl.when(d > 0)
                    def _():
                        g_copy(d + k, c, False).start()
        if step == 1:
            x_local.wait()
            for i in range(1, n):
                source = lax.rem(d + i, n)
                pltpu.make_async_remote_copy(
                    src_ref=xbuf.at[t, source], dst_ref=xbuf.at[t, source], send_sem=x_send.at[0],
                    recv_sem=x_recv.at[source], device_id={"dp": source}, device_id_type=MESH).wait_recv()
            for j in range(1, m):
                peer = lax.rem(t + j, m)
                copy = pltpu.make_async_remote_copy(
                    src_ref=xbuf.at[t], dst_ref=xbuf.at[t], send_sem=xt_send.at[j], recv_sem=xt_recv.at[t],
                    device_id={"tp": peer}, device_id_type=MESH)
                copy.start()
                x_tp.append(copy)
        if step == n - 1:
            for j in range(1, m):
                peer = lax.rem(t + j, m)
                pltpu.make_async_remote_copy(
                    src_ref=xbuf.at[peer], dst_ref=xbuf.at[peer], send_sem=xt_send.at[0],
                    recv_sem=xt_recv.at[peer], device_id={"tp": peer}, device_id_type=MESH).wait_recv()
            rows = [xbuf[j, r].astype(jnp.float32) for r in range(n) for j in range(m)]
            x_out[...] = jnp.concatenate(rows, axis=0).astype(jnp.bfloat16)
        done = step - (n - 1)
        if done >= 0:
            lo, hi = chunks[done]
            cols = pl.ds(lo, hi - lo)
            pltpu.make_async_copy(gbuf.at[:, :, cols], g_out.at[:, :, cols], out_sem.at[done]).start()
            hi = min(hi, width)
            w_loads[done].wait()
            grads = gbuf[:, :, lo:hi].reshape(n * tokens, hi - lo)
            acc[...] += lax.dot_general(
                grads, wbuf[lo:hi, :], (((1,), (0,)), ((), ())), preferred_element_type=jnp.float32)
    def pass_copy(i, j):
        return pltpu.make_async_remote_copy(
            src_ref=pbuf.at[j * n + i], dst_ref=rbuf.at[j * n + i],
            send_sem=p_send.at[j * n + i], recv_sem=p_recv.at[j * n + i],
            device_id=owner_of(p - 1, i, j), device_id_type=MESH)

    for i, j in everyone:
        start = lax.rem(d + i, n) * tokens + lax.rem(t + j, m) * own_rows
        rows = acc[pl.ds(pl.multiple_of(start, own_rows), own_rows), :]
        pbuf[j * n + i] = rows.astype(jnp.bfloat16)

    @pl.when(p > 0)
    def _():
        for i, j in everyone:
            pass_copy(i, j).start()

    for copy in x_copies + x_tp:
        copy.wait_send()
    for c, (lo, hi) in enumerate(chunks):
        cols = pl.ds(lo, hi - lo)
        pltpu.make_async_copy(gbuf.at[:, :, cols], g_out.at[:, :, cols], out_sem.at[c]).wait()
        for k in range(n):
            @pl.when((d - k >= 0) & (d < n - 1))
            def _():
                g_copy(d - k, c, True).wait_send()

            @pl.when((d + k < n) & (d > 0))
            def _():
                g_copy(d + k, c, False).wait_send()


    @pl.when(p < n_pp - 1)
    def _():
        for i, j in everyone:
            pass_copy(i, j).wait_recv()
        for i in range(n):
            total = rbuf[i].astype(jnp.float32)
            for j in range(1, m):
                total += rbuf[j * n + i].astype(jnp.float32)
            source = lax.rem(d - i + n, n)
            passed_out[:, pl.ds(pl.multiple_of(source * feats, LANES), feats)] = total.astype(jnp.bfloat16)

    @pl.when(p == n_pp - 1)
    def _():
        passed_out[...] = jnp.zeros_like(passed_out)

    @pl.when(p > 0)
    def _():
        for i, j in everyone:
            pass_copy(i, j).wait_send()


def weight_kernel(x_ref, g_ref, passed_ref, out_ref, passed_out):
    passed_out[...] = passed_ref[...]
    out_ref[...] = lax.dot_general(
        g_ref[...], x_ref[...], (((0,), (0,)), ((), ())), preferred_element_type=jnp.float32
    ).astype(out_ref.dtype)


def on_device(n_pp, n_tp, n_dp, layer_input, gate_pre, up_pre, hidden_grad, gate_weight):
    n, m = n_dp, n_tp
    tokens, width = gate_pre.shape[2:]
    own_rows, feats_all = layer_input.shape[2:]
    weights_t = jnp.swapaxes(gate_weight, 1, 2)
    feats = gate_weight.shape[1]
    padded = round_up(width, LANES)
    chunks = chunk_list(padded, 20)
    bf16, f32 = jnp.bfloat16, jnp.float32
    vmem, hbm = pltpu.VMEM, pl.BlockSpec(memory_space=pltpu.HBM)
    dma = pltpu.SemaphoreType.DMA
    results = pl.pallas_call(
        functools.partial(gather_kernel, n_pp, n, m, chunks),
        out_shape=[jax.ShapeDtypeStruct((n, tokens, padded), bf16), jax.ShapeDtypeStruct((n * tokens, feats), bf16)]
        + [jax.ShapeDtypeStruct((own_rows, feats_all), bf16)],
        in_specs=[hbm] * 5,
        out_specs=[pl.BlockSpec(memory_space=pl.ANY)] + [pl.BlockSpec(memory_space=vmem)] * 2,
        scratch_shapes=[
            dma((n * m,)), dma((n * m,)),
            vmem((n * m, own_rows, feats), bf16), vmem((n * m, own_rows, feats), bf16),
            vmem((own_rows, feats_all), bf16),
            vmem((tokens, width), bf16), vmem((tokens, width), bf16), vmem((tokens, width), bf16),
            vmem((width, feats), bf16),
            vmem((n, tokens, padded), bf16),
            vmem((m, n, own_rows, feats), bf16),
            vmem((n * tokens, feats), f32),
            dma((4,)), dma((len(chunks),)), dma((len(chunks) + 1,)),
            dma((n,)), dma((n,)), dma((m,)), dma((m,)),
            dma((n, len(chunks))), dma((n, len(chunks))), dma((n, len(chunks))),
        ],
        compiler_params=pltpu.CompilerParams(
            collective_id=0, has_side_effects=True, vmem_limit_bytes=58 * 1024 * 1024),
        cost_estimate=pl.CostEstimate(flops=2 * n * tokens * width * feats, bytes_accessed=16 * feats * width, transcendentals=0),
        name="gather",
    )(layer_input, gate_pre, up_pre, hidden_grad, weights_t)
    g_all, x_all, passed = results

    block = min(2048, padded)
    weight_out, passed = pl.pallas_call(
        weight_kernel,
        grid=(pl.cdiv(width, block),),
        out_shape=[jax.ShapeDtypeStruct((width, feats), bf16), jax.ShapeDtypeStruct((own_rows, feats_all), bf16)],
        in_specs=[
            pl.BlockSpec((n * tokens, feats), lambda i: (0, 0)),
            pl.BlockSpec((n * tokens, block), lambda i: (0, i)),
            pl.BlockSpec((own_rows, feats_all), lambda i: (0, 0)),
        ],
        out_specs=[pl.BlockSpec((block, feats), lambda i: (i, 0)), pl.BlockSpec((own_rows, feats_all), lambda i: (0, 0))],
        cost_estimate=pl.CostEstimate(flops=8 * n * tokens * width * feats, bytes_accessed=2 * feats * width, transcendentals=0),
        compiler_params=pltpu.CompilerParams(vmem_limit_bytes=58 * 1024 * 1024),
        name="weights",
    )(x_all, g_all.reshape(n * tokens, padded), passed)

    return passed[None, None], jnp.swapaxes(weight_out, 0, 1)[None]


def solution(mesh):
    return jax.shard_map(
        functools.partial(on_device, mesh.shape["pp"], mesh.shape["tp"], mesh.shape["dp"]),
        mesh=mesh,
        in_specs=(
            P("pp", "dp", "tp", None),
            P("pp", "dp", None, "tp"),
            P("pp", "dp", None, "tp"),
            P("pp", "dp", None, "tp"),
            P("pp", "dp", "tp"),
        ),
        out_specs=(P("pp", "dp", "tp", None), P("pp", "dp", "tp")),
        check_vma=False,
    )
```

time: 124 us -> 43 us (0.35)
  the two profiles are of different devices: /device:TPU:0 before, /device:TPU:1 now
where the time goes in v1:
time: 43 us; the launch traced here: 42.8 us
  Pallas kernels  42.2 us (98%)
  between operations  0.64 us (1%)
    pallas_call x1, Pallas kernels, on_device(): pl.pallas_call(functools.partial(gather_kernel, n_pp, n, m, chunks), out_...  33.7 us
    pallas_call x1, Pallas kernels, on_device(): pl.pallas_call(weight_kernel, grid=(pl.cdiv(width, block),), out_shape=[j...  8.47 us

profile of v1, /device:TPU:1, one launch (start us, length us, event | category | flops | bytes accessed | tf_op | source)
XLA Modules:
  0.0 42.8 jit_solution(12712689176511187739)
XLA Ops:
  0.6 33.7 %gather.1 = (bf16[4,16,7424]{2,1,0:T(8,128)(2,1)}, bf16[64,1024]{1,0:T(8,128)(2,1)}, bf16[8,4096]{1,0:T(8,128)(2,1)}) custom-call(bf16[1,1,8,4096]{3,2,1,0:T(8,128)(2,1)} %x_hbm.1, bf16[1,1,16,7392]{3,2,1,0:T(8,128)(2,1)} %g_hbm.1, bf16[1,1,16,7392]{3,2,1,0:T(8,128)(2,1)} %u_hbm.1, bf16[1,1,16,7392]{3,2,1,0:T(8,128)(2,1)} %h_hbm.1, ...), custom_call_target="tpu_custom_call" | custom-call | flops 968884224 | bytes 121110528 | tf_op jit(solution)/shard_map/gather/pallas_call | solution.py:237
  34.4 8.5 %weights.1 = (bf16[7392,1024]{1,0:T(8,128)(2,1)}, bf16[8,4096]{1,0:T(8,128)(2,1)}) custom-call(bf16[64,1024]{1,0:T(8,128)(2,1)} %get-tuple-element.7.x_ref, bf16[64,7424]{1,0:T(8,128)(2,1)} %bitcast.7, bf16[8,4096]{1,0:T(8,128)(2,1)} %get-tuple-element.9.passed_ref), custom_call_target="tpu_custom_call" | custom-call | flops 3875536896 | bytes 15138816 | tf_op jit(solution)/shard_map/weights/pallas_call | solution.py:264
